TPU v7x, 32 devices: a whole 2x2x4 slice. The times are simulated.
32 devices in a mesh: lat: 8 (over y, x, core), lon: 4 (over z).
Axes of the slice: x: 2, y: 2, z: 4, core: 2. Of those that a mesh axis runs over, the one named last changes fastest.
Arguments:
- current: bfloat16 [69, 256, 512], P(None, 'lat', 'lon')
- next_fields: bfloat16 [96, 256, 512], P(('lat', 'lon')), may hold values from -6 to 6
- reader_slot: int32 [69], replicated, may hold values from 0 to 95, as said below
- first_weight: bfloat16 [9, 256, 69], replicated, may hold values from -0.25 to 0.25
- first_bias: float32 [256], replicated, may hold values from -3 to 3
- second_weight: bfloat16 [9, 256, 256], replicated, may hold values from -0.125 to 0.125
- second_bias: float32 [256], replicated, may hold values from -3 to 3
Outputs:
- features: bfloat16 [256, 256, 512], P(None, 'lat', 'lon')
- next_tile: bfloat16 [69, 256, 512], P(None, 'lat', 'lon')
Inputs may be any that keep to these rules, and one draw needn't show every extreme that they name: `reader_slot`: the 69 entries are different slots.
All inputs are finite; a program needn't handle non-finite values.
Results may differ from a plain program's by a relative error of at most 0.0053.
Values may be sent and summed in bfloat16 or wider, within the bound.
A program may use at most 128 MiB of HBM per device.

v0:
```python
import jax
import jax.numpy as jnp
from jax import lax
from jax.sharding import PartitionSpec as P


def padded_2(block, sides, width, periodic):
    for axis, dim in sides:
        count = lax.axis_size(axis)
        forward = [(i, i + 1) for i in range(count - 1)]
        if periodic:
            forward.append((count - 1, 0))
        backward = [(target, source) for source, target in forward]
        low = lax.ppermute(
            lax.slice_in_dim(block, block.shape[dim] - width, None, axis=dim), axis, forward
        )
        high = lax.ppermute(lax.slice_in_dim(block, 0, width, axis=dim), axis, backward)
        block = jnp.concatenate([low, block, high], axis=dim)
    return block


def conv_valid(padded, weight, bias):
    rows = padded.shape[1] - 2
    cols = padded.shape[2] - 2
    total = jnp.zeros((weight.shape[1], rows, cols), jnp.float32)
    for tap in range(9):
        shifted = padded[:, tap // 3 : tap // 3 + rows, tap % 3 : tap % 3 + cols]
        total = total + jnp.einsum(
            "ok,khw->ohw", weight[tap], shifted, preferred_element_type=jnp.float32
        )
    return total + bias[:, None, None]


def regrid(next_fields, reader_slot):
    slot_dev, rows_all, cols_all = next_fields.shape
    n_lat = lax.axis_size("lat")
    n_lon = lax.axis_size("lon")
    lat_rows = rows_all // n_lat
    lon_cols = cols_all // n_lon
    blocks = next_fields.reshape(slot_dev, n_lat, lat_rows, n_lon, lon_cols)
    ordered = blocks.transpose(1, 3, 0, 2, 4).reshape(n_lat * n_lon, slot_dev, lat_rows, lon_cols)
    moved = lax.all_to_all(ordered, ("lat", "lon"), split_axis=0, concat_axis=1, tiled=True)
    moved = moved.reshape(n_lat * n_lon * slot_dev, lat_rows, lon_cols)
    return jnp.take(moved, reader_slot, axis=0)


def encode(current, first_weight, first_bias, second_weight, second_bias):
    values = current.astype(jnp.float32)
    lat_rows = values.shape[1]
    lon_cols = values.shape[2]
    cells = lat_rows * lax.axis_size("lat") * lon_cols * lax.axis_size("lon")
    total, squares = lax.psum(
        (jnp.sum(values, axis=(1, 2)), jnp.sum(values * values, axis=(1, 2))), ("lat", "lon")
    )
    mean = total / cells
    scale = 1.0 / jnp.sqrt(squares / cells - mean * mean + 1e-05)
    normed = ((values - mean[:, None, None]) * scale[:, None, None]).astype(jnp.bfloat16)
    tall = padded_2(normed, (("lat", 1),), 2, False)
    padded = padded_2(tall, (("lon", 2),), 2, True)
    hidden = jax.nn.gelu(conv_valid(padded, first_weight, first_bias), approximate=True)
    global_row = lax.axis_index("lat") * lat_rows + jnp.arange(lat_rows + 2, dtype=jnp.int32) - 1
    inside = (global_row >= 0) & (global_row < lat_rows * lax.axis_size("lat"))
    hidden = jnp.where(inside[None, :, None], hidden, 0.0).astype(jnp.bfloat16)
    return conv_valid(hidden, second_weight, second_bias).astype(jnp.bfloat16)


def body(current, next_fields, reader_slot, first_weight, first_bias, second_weight, second_bias):
    features = encode(current, first_weight, first_bias, second_weight, second_bias)
    next_tile = regrid(next_fields, reader_slot)
    return (features, next_tile)


def solution(mesh):
    in_specs = (P(None, "lat", "lon"), P(("lat", "lon"), None, None), P(), P(), P(), P(), P())
    out_specs = (P(None, "lat", "lon"), P(None, "lat", "lon"))
    return jax.shard_map(body, mesh=mesh, in_specs=in_specs, out_specs=out_specs, check_vma=False)
```

profile of v0, /device:TPU:8, one launch (start us, length us, event | category | flops | bytes accessed | tf_op | source)
XLA Modules:
  0.0 147.3 jit_solution(17535352118714095713)
XLA Ops:
  0.6 1.8 %copy.13 = bf16[69,32,128]{0,2,1:T(8,128)(2,1)S(1)} copy(bf16[69,32,128]{2,1,0:T(8,128)(2,1)} %param.7) | data formatting | bytes 1130496 | tf_op args[0]
  2.5 0.6 convert_reduce_fusion
  3.1 40.4 %all-reduce = (f32[69]{0:T(128)S(1)}, f32[69]{0:T(128)S(1)}) all-reduce(f32[69]{0:T(128)S(1)} %get-tuple-element.9, f32[69]{0:T(128)S(1)} %get-tuple-element.8), channel_id=1, replica_groups=mesh['lat'=8,'lon'=4] {'lat','lon'}, use_global_device_ids=true, to_apply=%region_3.0 | all-reduce | flops 138 | bytes 1104 | tf_op jit(solution)/shard_map/psum | solution.py:52
  43.9 1.3 collective-permute-start
  45.2 1.3 collective-permute-start.1
  46.7 1.1 copy.14
  47.7 8.6 %all-to-all-start = ((bf16[32,3,32,128]{3,2,1,0:T(8,128)(2,1)}), bf16[32,3,32,128]{3,2,1,0:T(8,128)(2,1)}, u32[]{:S(2)}, u32[]{:S(2)}) async-start(bf16[32,3,32,128]{3,2,1,0:T(8,128)(2,1)} %bitcast.39), calls=%async_computation | async-start | bytes 1572864 | tf_op jit(solution)/shard_map/all_to_all | solution.py:42
  56.5 0.4 collective-permute-start.3
  56.8 1.7 %collective-permute-start.2 = (bf16[69,36,2]{0,2,1:T(2,128)(2,1)S(1)}, bf16[69,36,2]{0,2,1:T(2,128)(2,1)S(1)}, u32[]{:S(2)}, u32[]{:S(2)}) collective-permute-start(bf16[69,36,2]{0,2,1:T(2,128)(2,1)S(1)} %get-tuple-element.12), channel_id=1, source_target_pairs={{0,1},{1,2},{2,3},{3,0},{4,5},{5,6},{6,7},{7,4},{8,9},{9,10},{10,1... | collective-permute-start | bytes 29816 | tf_op jit(solution)/shard_map/ppermute | solution.py:14
  58.5 17.9 %collective-permute-done.3 = bf16[69,36,2]{0,2,1:T(2,128)(2,1)S(1)} collective-permute-done((bf16[69,36,2]{0,2,1:T(2,128)(2,1)S(1)}, bf16[69,36,2]{0,2,1:T(2,128)(2,1)S(1)}, u32[]{:S(2)}, u32[]{:S(2)}) %collective-permute-start.3) | collective-permute-done | bytes 9968 | tf_op jit(solution)/shard_map/ppermute | solution.py:17
  76.4 0.5 pad_maximum_fusion
  76.9 0.8 fusion.32
  77.7 3.0 %fusion.34 = f32[34,130,256]{2,1,0:T(8,128)} fusion(bf16[69,36,132]{0,2,1:T(8,128)(2,1)S(1)} %pad_maximum_fusion, bf16[9,256,69]{1,2,0:T(8,128)(2,1)S(1)} %copy-done.2), kind=kOutput, calls=%fused_computation.41 | convolution fusion | flops 156149760 | bytes 5746688 | tf_op jit(solution)/shard_map/ok,khw->ohw/dot_general | solution.py:28
  80.7 2.9 %fusion.36 = f32[34,130,256]{2,1,0:T(8,128)} fusion(bf16[69,36,132]{0,2,1:T(8,128)(2,1)S(1)} %pad_maximum_fusion, bf16[9,256,69]{1,2,0:T(8,128)(2,1)S(1)} %copy-done.2), kind=kOutput, calls=%fused_computation.43 | convolution fusion | flops 156149760 | bytes 5746688 | tf_op jit(solution)/shard_map/ok,khw->ohw/dot_general | solution.py:28
  83.6 2.9 %fusion.63 = f32[34,130,256]{2,1,0:T(8,128)} fusion(bf16[9,256,69]{1,2,0:T(8,128)(2,1)S(1)} %copy-done.2, bf16[69,36,2]{0,2,1:T(2,128)(2,1)S(1)} %collective-permute-done.3, bf16[69,2,128]{0,2,1:T(8,128)(2,1)S(1)} %collective-permute-done.1, bf16[69,32,128]{0,2,1:T(8,128)(2,1)S(1)} %fusion.10, bf16[69,2,128]{0,2,1:T(8,128)(2,1)S(1)} %collective-permute-done), kind=kOutput, calls=%fused_computation.69 | convolution fusion | flops 158733120 | bytes 5761024 | tf_op jit(solution)/shard_map/ok,khw->ohw/dot_general | solution.py:28
  86.5 2.9 %fusion.66 = f32[34,130,256]{2,1,0:T(8,128)} fusion(bf16[9,256,69]{1,2,0:T(8,128)(2,1)S(1)} %copy-done.2, bf16[69,2,128]{0,2,1:T(8,128)(2,1)S(1)} %collective-permute-done.1, bf16[69,32,128]{0,2,1:T(8,128)(2,1)S(1)} %fusion.10, bf16[69,2,128]{0,2,1:T(8,128)(2,1)S(1)} %collective-permute-done, bf16[69,36,2]{0,2,1:T(2,128)(2,1)S(1)} %collective-permute-done.2), kind=kOutput, calls=%fused_computation.72 | convolution fusion | flops 158733120 | bytes 5761024 | tf_op jit(solution)/shard_map/ok,khw->ohw/dot_general | solution.py:28
  89.4 3.0 %fusion.68 = f32[34,130,256]{2,1,0:T(8,128)} fusion(bf16[9,256,69]{1,2,0:T(8,128)(2,1)S(1)} %copy-done.2, bf16[69,36,2]{0,2,1:T(2,128)(2,1)S(1)} %collective-permute-done.3, bf16[69,2,128]{0,2,1:T(8,128)(2,1)S(1)} %collective-permute-done.1, bf16[69,32,128]{0,2,1:T(8,128)(2,1)S(1)} %fusion.10, bf16[69,2,128]{0,2,1:T(8,128)(2,1)S(1)} %collective-permute-done), kind=kOutput, calls=%fused_computation.74 | convolution fusion | flops 158733120 | bytes 5761024 | tf_op jit(solution)/shard_map/ok,khw->ohw/dot_general | solution.py:28
  92.4 3.0 %fusion.71 = f32[34,130,256]{2,1,0:T(8,128)} fusion(bf16[9,256,69]{1,2,0:T(8,128)(2,1)S(1)} %copy-done.2, bf16[69,2,128]{0,2,1:T(8,128)(2,1)S(1)} %collective-permute-done.1, bf16[69,32,128]{0,2,1:T(8,128)(2,1)S(1)} %fusion.10, bf16[69,2,128]{0,2,1:T(8,128)(2,1)S(1)} %collective-permute-done, bf16[69,36,2]{0,2,1:T(2,128)(2,1)S(1)} %collective-permute-done.2), kind=kOutput, calls=%fused_computation.77 | convolution fusion | flops 158733120 | bytes 5761024 | tf_op jit(solution)/shard_map/ok,khw->ohw/dot_general | solution.py:28
  95.4 2.9 %fusion.61 = f32[34,130,256]{2,1,0:T(8,128)} fusion(bf16[9,256,69]{1,2,0:T(8,128)(2,1)S(1)} %copy-done.2, bf16[69,2,128]{0,2,1:T(8,128)(2,1)S(1)} %collective-permute-done.1, bf16[69,32,128]{0,2,1:T(8,128)(2,1)S(1)} %fusion.10, bf16[69,2,128]{0,2,1:T(8,128)(2,1)S(1)} %collective-permute-done, bf16[69,36,2]{0,2,1:T(2,128)(2,1)S(1)} %collective-permute-done.2), kind=kOutput, calls=%fused_computation.67 | convolution fusion | flops 158733120 | bytes 5761024 | tf_op jit(solution)/shard_map/ok,khw->ohw/dot_general | solution.py:28
  98.3 12.7 %fusion.8 = bf16[256,34,130]{0,2,1:T(8,128)(2,1)S(1)} fusion(f32[34,130,256]{2,1,0:T(8,128)S(1)} %fusion.32, f32[34,130,256]{2,1,0:T(8,128)} %fusion.61, f32[34,130,256]{2,1,0:T(8,128)} %fusion.63, f32[34,130,256]{2,1,0:T(8,128)} %fusion.34, f32[34,130,256]{2,1,0:T(8,128)} %fusion.66, f32[34,130,256]{2,1,0:T(8,128)} %fusion.68, ...), kind=kOutput, calls=%fused_computation.10 | convolution fusion | flops 180232000 | bytes 39917056 | tf_op jit(solution)/shard_map/ok,khw->ohw/dot_general | solution.py:28
  111.0 0.8 fusion.13
  111.7 2.7 %fusion.15 = f32[32,128,256]{2,1,0:T(8,128)} fusion(bf16[256,34,130]{0,2,1:T(8,128)(2,1)S(1)} %fusion.8, bf16[9,256,256]{2,1,0:T(8,128)(2,1)S(1)} %copy-done), kind=kOutput, calls=%fused_computation.21 | convolution fusion | flops 536870912 | bytes 6422528 | tf_op jit(solution)/shard_map/ok,khw->ohw/dot_general | solution.py:28
  114.4 2.7 %fusion.17 = f32[32,128,256]{2,1,0:T(8,128)} fusion(bf16[256,34,130]{0,2,1:T(8,128)(2,1)S(1)} %fusion.8, bf16[9,256,256]{2,1,0:T(8,128)(2,1)S(1)} %copy-done), kind=kOutput, calls=%fused_computation.23 | convolution fusion | flops 536870912 | bytes 6422528 | tf_op jit(solution)/shard_map/ok,khw->ohw/dot_general | solution.py:28
  117.2 2.7 %fusion.19 = f32[32,128,256]{2,1,0:T(8,128)} fusion(bf16[256,34,130]{0,2,1:T(8,128)(2,1)S(1)} %fusion.8, bf16[9,256,256]{2,1,0:T(8,128)(2,1)S(1)} %copy-done), kind=kOutput, calls=%fused_computation.25 | convolution fusion | flops 536870912 | bytes 6422528 | tf_op jit(solution)/shard_map/ok,khw->ohw/dot_general | solution.py:28
  119.9 2.7 %fusion.21 = f32[32,128,256]{2,1,0:T(8,128)} fusion(bf16[256,34,130]{0,2,1:T(8,128)(2,1)S(1)} %fusion.8, bf16[9,256,256]{2,1,0:T(8,128)(2,1)S(1)} %copy-done), kind=kOutput, calls=%fused_computation.27 | convolution fusion | flops 536870912 | bytes 6422528 | tf_op jit(solution)/shard_map/ok,khw->ohw/dot_general | solution.py:28
  122.6 2.7 %fusion.23 = f32[32,128,256]{2,1,0:T(8,128)} fusion(bf16[256,34,130]{0,2,1:T(8,128)(2,1)S(1)} %fusion.8, bf16[9,256,256]{2,1,0:T(8,128)(2,1)S(1)} %copy-done), kind=kOutput, calls=%fused_computation.29 | convolution fusion | flops 536870912 | bytes 6422528 | tf_op jit(solution)/shard_map/ok,khw->ohw/dot_general | solution.py:28
  125.3 2.7 %fusion.25 = f32[32,128,256]{2,1,0:T(8,128)} fusion(bf16[256,34,130]{0,2,1:T(8,128)(2,1)S(1)} %fusion.8, bf16[9,256,256]{2,1,0:T(8,128)(2,1)S(1)} %copy-done), kind=kOutput, calls=%fused_computation.31 | convolution fusion | flops 536870912 | bytes 6422528 | tf_op jit(solution)/shard_map/ok,khw->ohw/dot_general | solution.py:28
  128.0 2.7 %fusion.27 = f32[32,128,256]{2,1,0:T(8,128)} fusion(bf16[256,34,130]{0,2,1:T(8,128)(2,1)S(1)} %fusion.8, bf16[9,256,256]{2,1,0:T(8,128)(2,1)S(1)} %copy-done), kind=kOutput, calls=%fused_computation.33 | convolution fusion | flops 536870912 | bytes 6422528 | tf_op jit(solution)/shard_map/ok,khw->ohw/dot_general | solution.py:28
  130.7 10.8 %fusion.29 = bf16[256,32,128]{0,2,1:T(8,128)(2,1)S(1)} fusion(f32[256]{0:T(256)S(1)} %copy-done.4, bf16[256,34,130]{0,2,1:T(8,128)(2,1)S(1)} %fusion.8, f32[32,128,256]{2,1,0:T(8,128)S(1)} %fusion.13, f32[32,128,256]{2,1,0:T(8,128)} %fusion.15, f32[32,128,256]{2,1,0:T(8,128)} %fusion.17, f32[32,128,256]{2,1,0:T(8,128)} %fusion.19, ...), kind=kOutput, calls=%fused_computation.35 | convolution fusion | flops 547356672 | bytes 37880832 | tf_op jit(solution)/shard_map/ok,khw->ohw/dot_general | solution.py:28
  141.5 3.1 %copy.15 = bf16[256,32,128]{2,1,0:T(8,128)(2,1)} copy(bf16[256,32,128]{0,2,1:T(8,128)(2,1)S(1)} %fusion.29) | data formatting | bytes 4194304
  144.5 1.8 %gather_fusion = bf16[69,32,128]{2,1,0:T(8,128)(2,1)S(1)} fusion(bf16[96,32,128]{2,1,0:T(8,128)(2,1)} %bitcast.40, s32[1024]{0:T(1024)S(1)} %pad_clamp_fusion), kind=kCustom, calls=%fused_computation | custom fusion | bytes 1130772 | tf_op jit(solution)/shard_map/jit(_take)/gather | solution.py:44
  146.3 1.0 broadcast_select_fusion
  (25 shorter events, 0.6 us)
Async XLA Ops:
  0.6 45.8 %copy-start.1 = (bf16[3,256,512]{2,1,0:T(8,128)(2,1)S(1)}, bf16[3,256,512]{2,1,0:T(8,128)(2,1)}, u32[]{:S(2)}) copy-start(bf16[3,256,512]{2,1,0:T(8,128)(2,1)} %param.8) | copy-start | bytes 2359300
  43.8 12.5 %copy-start.5 = (s32[69]{0:T(128)S(1)}, s32[69]{0:T(128)}, u32[]{:S(2)}) copy-start(s32[69]{0:T(128)} %param.9) | copy-start | bytes 832
  43.9 12.5 %collective-permute-start = (bf16[69,2,128]{0,2,1:T(8,128)(2,1)S(1)}, bf16[69,2,128]{0,2,1:T(8,128)(2,1)S(1)}, u32[]{:S(2)}, u32[]{:S(2)}) collective-permute-start(bf16[69,2,128]{0,2,1:T(8,128)(2,1)S(1)} %get-tuple-element.14), channel_id=1, source_target_pairs={{0,4},{4,8},{8,12},{12,16},{16,20},{20,24},{24,28},{1,5},{5,9},{9,... | collective-permute-start | bytes 105992 | tf_op jit(solution)/shard_map/ppermute | solution.py:14
  45.2 11.2 %collective-permute-start.1 = (bf16[69,2,128]{0,2,1:T(8,128)(2,1)S(1)}, bf16[69,2,128]{0,2,1:T(8,128)(2,1)S(1)}, u32[]{:S(2)}, u32[]{:S(2)}) collective-permute-start(bf16[69,2,128]{0,2,1:T(8,128)(2,1)S(1)} %get-tuple-element.15), channel_id=1, source_target_pairs={{4,0},{8,4},{12,8},{16,12},{20,16},{24,20},{28,24},{5,1},{9,5},{13... | collective-permute-start | bytes 105992 | tf_op jit(solution)/shard_map/ppermute | solution.py:17
  47.7 29.2 %copy-start.2 = (bf16[9,256,69]{1,2,0:T(8,128)(2,1)S(1)}, bf16[9,256,69]{1,2,0:T(8,128)(2,1)}, u32[]{:S(2)}) copy-start(bf16[9,256,69]{1,2,0:T(8,128)(2,1)} %param.10) | copy-start | bytes 953860
  47.7 96.8 %all-to-all-start = ((bf16[32,3,32,128]{3,2,1,0:T(8,128)(2,1)}), bf16[32,3,32,128]{3,2,1,0:T(8,128)(2,1)}, u32[]{:S(2)}, u32[]{:S(2)}) async-start(bf16[32,3,32,128]{3,2,1,0:T(8,128)(2,1)} %bitcast.39), calls=%async_computation | async-start | bytes 1572864 | tf_op jit(solution)/shard_map/all_to_all | solution.py:42
  56.5 20.0 %collective-permute-start.3 = (bf16[69,36,2]{0,2,1:T(2,128)(2,1)S(1)}, bf16[69,36,2]{0,2,1:T(2,128)(2,1)S(1)}, u32[]{:S(2)}, u32[]{:S(2)}) collective-permute-start(bf16[69,36,2]{0,2,1:T(2,128)(2,1)S(1)} %get-tuple-element.13), channel_id=1, source_target_pairs={{1,0},{2,1},{3,2},{0,3},{5,4},{6,5},{7,6},{4,7},{9,8},{10,9},{11,1... | collective-permute-start | bytes 29816 | tf_op jit(solution)/shard_map/ppermute | solution.py:17
  56.8 19.6 %collective-permute-start.2 = (bf16[69,36,2]{0,2,1:T(2,128)(2,1)S(1)}, bf16[69,36,2]{0,2,1:T(2,128)(2,1)S(1)}, u32[]{:S(2)}, u32[]{:S(2)}) collective-permute-start(bf16[69,36,2]{0,2,1:T(2,128)(2,1)S(1)} %get-tuple-element.12), channel_id=1, source_target_pairs={{0,1},{1,2},{2,3},{3,0},{4,5},{5,6},{6,7},{7,4},{8,9},{9,10},{10,1... | collective-permute-start | bytes 29816 | tf_op jit(solution)/shard_map/ppermute | solution.py:14
  95.4 2.9 %copy-start.3 = (f32[256]{0:T(256)S(1)}, f32[256]{0:T(256)}, u32[]{:S(2)}) copy-start(f32[256]{0:T(256)} %param.11) | copy-start | bytes 3076
  98.3 12.7 %copy-start = (bf16[9,256,256]{2,1,0:T(8,128)(2,1)S(1)}, bf16[9,256,256]{2,1,0:T(8,128)(2,1)}, u32[]{:S(2)}) copy-start(bf16[9,256,256]{2,1,0:T(8,128)(2,1)} %param.12) | copy-start | bytes 3538948
  128.0 2.7 %copy-start.4 = (f32[256]{0:T(256)S(1)}, f32[256]{0:T(256)}, u32[]{:S(2)}) copy-start(f32[256]{0:T(256)} %param.13) | copy-start | bytes 3076
where the time goes:
time: 148 us; the launch traced here: 147 us
  matrix products  64.5 us (44%)
  blocking collectives  40.4 us (27%)
  waiting for transfers between devices  17.9 us (12%)
  starting transfers between devices  13.3 us (9%)
  local copies, waits for them, and re-layouts  7.99 us (5%)
  other arithmetic  2.36 us (2%)
    dot_general x18, matrix products, conv_valid(): jnp.einsum('ok,khw->ohw', weight[tap], shifted, preferred_element_type=jn...  64.5 us
    psum x1, blocking collectives, encode(): lax.psum((jnp.sum(values, axis=(1, 2)), jnp.sum(values * values, axis=(1,...  40.4 us
    ppermute x2, waiting for transfers between devices, padded_2(): lax.ppermute(lax.slice_in_dim(block, 0, width, axis=dim), axis, backward)  17.9 us
    all_to_all x1, starting transfers between devices, regrid(): lax.all_to_all(ordered, ('lat', 'lon'), split_axis=0, concat_axis=1, tile...  8.59 us
    unnamed x14, local copies, waits for them, and re-layouts  4.93 us
    ppermute x2, starting transfers between devices, padded_2(): lax.ppermute(lax.slice_in_dim(block, block.shape[dim] - width, None, axis...  3 us
  transfers between devices with their start and end apart: 5, of which 1 were waited for; matrix products, arithmetic and copies ran while one was open for 47% of the time, Pallas kernels for 0%

commit v1 on v0

--- a/solution.py
+++ b/solution.py
@@ -2,6 +2,11 @@
 import jax.numpy as jnp
 from jax import lax
 from jax.sharding import PartitionSpec as P
+
+
+def by_each_axis(x, first, second):
+    half = lax.psum(x, first)
+    return lax.psum(half, second)
 
 
 def padded_2(block, sides, width, periodic):
@@ -49,8 +54,8 @@
     lat_rows = values.shape[1]
     lon_cols = values.shape[2]
     cells = lat_rows * lax.axis_size("lat") * lon_cols * lax.axis_size("lon")
-    total, squares = lax.psum(
-        (jnp.sum(values, axis=(1, 2)), jnp.sum(values * values, axis=(1, 2))), ("lat", "lon")
+    total, squares = by_each_axis(
+        (jnp.sum(values, axis=(1, 2)), jnp.sum(values * values, axis=(1, 2))), "lon", "lat"
     )
     mean = total / cells
     scale = 1.0 / jnp.sqrt(squares / cells - mean * mean + 1e-05)

time: 148 us -> 128 us (0.86)
  blocking collectives: 40.4 us -> 20.9 us
    psum x1 -> x2, blocking collectives: 40.4 us -> 20.9 us  [the longest x1 11.9 us: by_each_axis(): return lax.psum(half, second)]
  transfers between devices with their start and end apart: 5 -> 5, of which waited for: 1 -> 1; matrix products, arithmetic and copies ran while one was open for 47% -> 54% of each run, Pallas kernels for 0% -> 0%
where the time goes in v1:
time: 128 us
  matrix products  64.5 us (50%)
  blocking collectives  20.9 us (16%)
  waiting for transfers between devices  17.9 us (14%)
  starting transfers between devices  13.6 us (11%)
  local copies, waits for them, and re-layouts  8 us (6%)
  other arithmetic  2.36 us (2%)
    dot_general x18, matrix products, conv_valid(): jnp.einsum('ok,khw->ohw', weight[tap], shifted, preferred_element_type=jn...  64.5 us
    ppermute x2, waiting for transfers between devices, padded_2(): lax.ppermute(lax.slice_in_dim(block, 0, width, axis=dim), axis, backward)  17.9 us
    psum x1, blocking collectives, by_each_axis(): return lax.psum(half, second)  11.9 us
    psum x1, blocking collectives, by_each_axis(): half = lax.psum(x, first)  9 us
    all_to_all x1, starting transfers between devices, regrid(): lax.all_to_all(ordered, ('lat', 'lon'), split_axis=0, concat_axis=1, tile...  8.59 us
    unnamed x14, local copies, waits for them, and re-layouts  4.93 us
    ppermute x2, starting transfers between devices, padded_2(): lax.ppermute(lax.slice_in_dim(block, block.shape[dim] - width, None, axis...  3.33 us
  transfers between devices with their start and end apart: 5, of which 1 were waited for; matrix products, arithmetic and copies ran while one was open for 54% of the time, Pallas kernels for 0%

profile of v1, /device:TPU:8, one launch (start us, length us, event | category | flops | bytes accessed | tf_op | source)
XLA Modules:
  0.0 128.2 jit_solution(5238870986373519348)
XLA Ops:
  0.6 1.8 %copy.13 = bf16[69,32,128]{0,2,1:T(8,128)(2,1)S(1)} copy(bf16[69,32,128]{2,1,0:T(8,128)(2,1)} %param.7) | data formatting | bytes 1130496 | tf_op args[0]
  2.5 0.6 convert_reduce_fusion
  3.1 9.0 %all-reduce.1 = (f32[69]{0:T(128)S(1)}, f32[69]{0:T(128)S(1)}) all-reduce(f32[69]{0:T(128)S(1)} %get-tuple-element.9, f32[69]{0:T(128)S(1)} %get-tuple-element.8), channel_id=1, replica_groups=mesh['lat'=8,'lon'=4] {'lon'}, use_global_device_ids=true, to_apply=%region_4.0 | all-reduce | flops 138 | bytes 1104 | tf_op jit(solution)/shard_map/psum | solution.py:8
  12.0 11.9 %all-reduce = (f32[69]{0:T(128)S(1)}, f32[69]{0:T(128)S(1)}) all-reduce(f32[69]{0:T(128)S(1)} %get-tuple-element.12, f32[69]{0:T(128)S(1)} %get-tuple-element.13), channel_id=1, replica_groups=mesh['lat'=8,'lon'=4] {'lat'}, use_global_device_ids=true, to_apply=%region_5.0 | all-reduce | flops 138 | bytes 1104 | tf_op jit(solution)/shard_map/psum | solution.py:9
  24.3 1.6 %collective-permute-start = (bf16[69,2,128]{0,2,1:T(8,128)(2,1)S(1)}, bf16[69,2,128]{0,2,1:T(8,128)(2,1)S(1)}, u32[]{:S(2)}, u32[]{:S(2)}) collective-permute-start(bf16[69,2,128]{0,2,1:T(8,128)(2,1)S(1)} %get-tuple-element.16), channel_id=1, source_target_pairs={{0,4},{4,8},{8,12},{12,16},{16,20},{20,24},{24,28},{1,5},{5,9},{9,... | collective-permute-start | bytes 105992 | tf_op jit(solution)/shard_map/ppermute | solution.py:19
  26.0 1.3 %collective-permute-start.1 = (bf16[69,2,128]{0,2,1:T(8,128)(2,1)S(1)}, bf16[69,2,128]{0,2,1:T(8,128)(2,1)S(1)}, u32[]{:S(2)}, u32[]{:S(2)}) collective-permute-start(bf16[69,2,128]{0,2,1:T(8,128)(2,1)S(1)} %get-tuple-element.17), channel_id=1, source_target_pairs={{4,0},{8,4},{12,8},{16,12},{20,16},{24,20},{28,24},{5,1},{9,5},{13... | collective-permute-start | bytes 105992 | tf_op jit(solution)/shard_map/ppermute | solution.py:22
  27.5 1.1 copy.14
  28.6 8.6 %all-to-all-start = ((bf16[32,3,32,128]{3,2,1,0:T(8,128)(2,1)}), bf16[32,3,32,128]{3,2,1,0:T(8,128)(2,1)}, u32[]{:S(2)}, u32[]{:S(2)}) async-start(bf16[32,3,32,128]{3,2,1,0:T(8,128)(2,1)} %bitcast.39), calls=%async_computation | async-start | bytes 1572864 | tf_op jit(solution)/shard_map/all_to_all | solution.py:47
  37.6 1.7 %collective-permute-start.2 = (bf16[69,36,2]{0,2,1:T(2,128)(2,1)S(1)}, bf16[69,36,2]{0,2,1:T(2,128)(2,1)S(1)}, u32[]{:S(2)}, u32[]{:S(2)}) collective-permute-start(bf16[69,36,2]{0,2,1:T(2,128)(2,1)S(1)} %get-tuple-element.14), channel_id=1, source_target_pairs={{0,1},{1,2},{2,3},{3,0},{4,5},{5,6},{6,7},{7,4},{8,9},{9,10},{10,1... | collective-permute-start | bytes 29816 | tf_op jit(solution)/shard_map/ppermute | solution.py:19
  39.4 17.9 %collective-permute-done.3 = bf16[69,36,2]{0,2,1:T(2,128)(2,1)S(1)} collective-permute-done((bf16[69,36,2]{0,2,1:T(2,128)(2,1)S(1)}, bf16[69,36,2]{0,2,1:T(2,128)(2,1)S(1)}, u32[]{:S(2)}, u32[]{:S(2)}) %collective-permute-start.3) | collective-permute-done | bytes 9968 | tf_op jit(solution)/shard_map/ppermute | solution.py:22
  57.3 0.5 pad_maximum_fusion
  57.7 0.8 fusion.32
  58.5 3.0 %fusion.34 = f32[34,130,256]{2,1,0:T(8,128)} fusion(bf16[69,36,132]{0,2,1:T(8,128)(2,1)S(1)} %pad_maximum_fusion, bf16[9,256,69]{1,2,0:T(8,128)(2,1)S(1)} %copy-done.2), kind=kOutput, calls=%fused_computation.41 | convolution fusion | flops 156149760 | bytes 5746688 | tf_op jit(solution)/shard_map/ok,khw->ohw/dot_general | solution.py:33
  61.5 2.9 %fusion.36 = f32[34,130,256]{2,1,0:T(8,128)} fusion(bf16[69,36,132]{0,2,1:T(8,128)(2,1)S(1)} %pad_maximum_fusion, bf16[9,256,69]{1,2,0:T(8,128)(2,1)S(1)} %copy-done.2), kind=kOutput, calls=%fused_computation.43 | convolution fusion | flops 156149760 | bytes 5746688 | tf_op jit(solution)/shard_map/ok,khw->ohw/dot_general | solution.py:33
  64.4 2.9 %fusion.63 = f32[34,130,256]{2,1,0:T(8,128)} fusion(bf16[9,256,69]{1,2,0:T(8,128)(2,1)S(1)} %copy-done.2, bf16[69,36,2]{0,2,1:T(2,128)(2,1)S(1)} %collective-permute-done.3, bf16[69,2,128]{0,2,1:T(8,128)(2,1)S(1)} %collective-permute-done.1, bf16[69,32,128]{0,2,1:T(8,128)(2,1)S(1)} %fusion.10, bf16[69,2,128]{0,2,1:T(8,128)(2,1)S(1)} %collective-permute-done), kind=kOutput, calls=%fused_computation.69 | convolution fusion | flops 158733120 | bytes 5761024 | tf_op jit(solution)/shard_map/ok,khw->ohw/dot_general | solution.py:33
  67.3 2.9 %fusion.66 = f32[34,130,256]{2,1,0:T(8,128)} fusion(bf16[9,256,69]{1,2,0:T(8,128)(2,1)S(1)} %copy-done.2, bf16[69,2,128]{0,2,1:T(8,128)(2,1)S(1)} %collective-permute-done.1, bf16[69,32,128]{0,2,1:T(8,128)(2,1)S(1)} %fusion.10, bf16[69,2,128]{0,2,1:T(8,128)(2,1)S(1)} %collective-permute-done, bf16[69,36,2]{0,2,1:T(2,128)(2,1)S(1)} %collective-permute-done.2), kind=kOutput, calls=%fused_computation.72 | convolution fusion | flops 158733120 | bytes 5761024 | tf_op jit(solution)/shard_map/ok,khw->ohw/dot_general | solution.py:33
  70.2 2.9 %fusion.68 = f32[34,130,256]{2,1,0:T(8,128)} fusion(bf16[9,256,69]{1,2,0:T(8,128)(2,1)S(1)} %copy-done.2, bf16[69,36,2]{0,2,1:T(2,128)(2,1)S(1)} %collective-permute-done.3, bf16[69,2,128]{0,2,1:T(8,128)(2,1)S(1)} %collective-permute-done.1, bf16[69,32,128]{0,2,1:T(8,128)(2,1)S(1)} %fusion.10, bf16[69,2,128]{0,2,1:T(8,128)(2,1)S(1)} %collective-permute-done), kind=kOutput, calls=%fused_computation.74 | convolution fusion | flops 158733120 | bytes 5761024 | tf_op jit(solution)/shard_map/ok,khw->ohw/dot_general | solution.py:33
  73.2 3.0 %fusion.71 = f32[34,130,256]{2,1,0:T(8,128)} fusion(bf16[9,256,69]{1,2,0:T(8,128)(2,1)S(1)} %copy-done.2, bf16[69,2,128]{0,2,1:T(8,128)(2,1)S(1)} %collective-permute-done.1, bf16[69,32,128]{0,2,1:T(8,128)(2,1)S(1)} %fusion.10, bf16[69,2,128]{0,2,1:T(8,128)(2,1)S(1)} %collective-permute-done, bf16[69,36,2]{0,2,1:T(2,128)(2,1)S(1)} %collective-permute-done.2), kind=kOutput, calls=%fused_computation.77 | convolution fusion | flops 158733120 | bytes 5761024 | tf_op jit(solution)/shard_map/ok,khw->ohw/dot_general | solution.py:33
  76.2 2.9 %fusion.61 = f32[34,130,256]{2,1,0:T(8,128)} fusion(bf16[9,256,69]{1,2,0:T(8,128)(2,1)S(1)} %copy-done.2, bf16[69,2,128]{0,2,1:T(8,128)(2,1)S(1)} %collective-permute-done.1, bf16[69,32,128]{0,2,1:T(8,128)(2,1)S(1)} %fusion.10, bf16[69,2,128]{0,2,1:T(8,128)(2,1)S(1)} %collective-permute-done, bf16[69,36,2]{0,2,1:T(2,128)(2,1)S(1)} %collective-permute-done.2), kind=kOutput, calls=%fused_computation.67 | convolution fusion | flops 158733120 | bytes 5761024 | tf_op jit(solution)/shard_map/ok,khw->ohw/dot_general | solution.py:33
  79.1 12.7 %fusion.8 = bf16[256,34,130]{0,2,1:T(8,128)(2,1)S(1)} fusion(f32[34,130,256]{2,1,0:T(8,128)S(1)} %fusion.32, f32[34,130,256]{2,1,0:T(8,128)} %fusion.61, f32[34,130,256]{2,1,0:T(8,128)} %fusion.63, f32[34,130,256]{2,1,0:T(8,128)} %fusion.34, f32[34,130,256]{2,1,0:T(8,128)} %fusion.66, f32[34,130,256]{2,1,0:T(8,128)} %fusion.68, ...), kind=kOutput, calls=%fused_computation.10 | convolution fusion | flops 180232000 | bytes 39917056 | tf_op jit(solution)/shard_map/ok,khw->ohw/dot_general | solution.py:33
  91.8 0.8 fusion.13
  92.6 2.7 %fusion.15 = f32[32,128,256]{2,1,0:T(8,128)} fusion(bf16[256,34,130]{0,2,1:T(8,128)(2,1)S(1)} %fusion.8, bf16[9,256,256]{2,1,0:T(8,128)(2,1)S(1)} %copy-done), kind=kOutput, calls=%fused_computation.21 | convolution fusion | flops 536870912 | bytes 6422528 | tf_op jit(solution)/shard_map/ok,khw->ohw/dot_general | solution.py:33
  95.3 2.7 %fusion.17 = f32[32,128,256]{2,1,0:T(8,128)} fusion(bf16[256,34,130]{0,2,1:T(8,128)(2,1)S(1)} %fusion.8, bf16[9,256,256]{2,1,0:T(8,128)(2,1)S(1)} %copy-done), kind=kOutput, calls=%fused_computation.23 | convolution fusion | flops 536870912 | bytes 6422528 | tf_op jit(solution)/shard_map/ok,khw->ohw/dot_general | solution.py:33
  98.0 2.7 %fusion.19 = f32[32,128,256]{2,1,0:T(8,128)} fusion(bf16[256,34,130]{0,2,1:T(8,128)(2,1)S(1)} %fusion.8, bf16[9,256,256]{2,1,0:T(8,128)(2,1)S(1)} %copy-done), kind=kOutput, calls=%fused_computation.25 | convolution fusion | flops 536870912 | bytes 6422528 | tf_op jit(solution)/shard_map/ok,khw->ohw/dot_general | solution.py:33
  100.7 2.7 %fusion.21 = f32[32,128,256]{2,1,0:T(8,128)} fusion(bf16[256,34,130]{0,2,1:T(8,128)(2,1)S(1)} %fusion.8, bf16[9,256,256]{2,1,0:T(8,128)(2,1)S(1)} %copy-done), kind=kOutput, calls=%fused_computation.27 | convolution fusion | flops 536870912 | bytes 6422528 | tf_op jit(solution)/shard_map/ok,khw->ohw/dot_general | solution.py:33
  103.4 2.7 %fusion.23 = f32[32,128,256]{2,1,0:T(8,128)} fusion(bf16[256,34,130]{0,2,1:T(8,128)(2,1)S(1)} %fusion.8, bf16[9,256,256]{2,1,0:T(8,128)(2,1)S(1)} %copy-done), kind=kOutput, calls=%fused_computation.29 | convolution fusion | flops 536870912 | bytes 6422528 | tf_op jit(solution)/shard_map/ok,khw->ohw/dot_general | solution.py:33
  106.1 2.7 %fusion.25 = f32[32,128,256]{2,1,0:T(8,128)} fusion(bf16[256,34,130]{0,2,1:T(8,128)(2,1)S(1)} %fusion.8, bf16[9,256,256]{2,1,0:T(8,128)(2,1)S(1)} %copy-done), kind=kOutput, calls=%fused_computation.31 | convolution fusion | flops 536870912 | bytes 6422528 | tf_op jit(solution)/shard_map/ok,khw->ohw/dot_general | solution.py:33
  108.8 2.7 %fusion.27 = f32[32,128,256]{2,1,0:T(8,128)} fusion(bf16[256,34,130]{0,2,1:T(8,128)(2,1)S(1)} %fusion.8, bf16[9,256,256]{2,1,0:T(8,128)(2,1)S(1)} %copy-done), kind=kOutput, calls=%fused_computation.33 | convolution fusion | flops 536870912 | bytes 6422528 | tf_op jit(solution)/shard_map/ok,khw->ohw/dot_general | solution.py:33
  111.6 10.8 %fusion.29 = bf16[256,32,128]{0,2,1:T(8,128)(2,1)S(1)} fusion(f32[256]{0:T(256)S(1)} %copy-done.4, bf16[256,34,130]{0,2,1:T(8,128)(2,1)S(1)} %fusion.8, f32[32,128,256]{2,1,0:T(8,128)S(1)} %fusion.13, f32[32,128,256]{2,1,0:T(8,128)} %fusion.15, f32[32,128,256]{2,1,0:T(8,128)} %fusion.17, f32[32,128,256]{2,1,0:T(8,128)} %fusion.19, ...), kind=kOutput, calls=%fused_computation.35 | convolution fusion | flops 547356672 | bytes 37880832 | tf_op jit(solution)/shard_map/ok,khw->ohw/dot_general | solution.py:33
  122.3 3.1 %copy.15 = bf16[256,32,128]{2,1,0:T(8,128)(2,1)} copy(bf16[256,32,128]{0,2,1:T(8,128)(2,1)S(1)} %fusion.29) | data formatting | bytes 4194304
  125.4 1.8 %gather_fusion = bf16[69,32,128]{2,1,0:T(8,128)(2,1)S(1)} fusion(bf16[96,32,128]{2,1,0:T(8,128)(2,1)} %bitcast.40, s32[1024]{0:T(1024)S(1)} %pad_clamp_fusion), kind=kCustom, calls=%fused_computation | custom fusion | bytes 1130772 | tf_op jit(solution)/shard_map/jit(_take)/gather | solution.py:49
  127.2 1.0 broadcast_select_fusion
  (26 shorter events, 1.0 us)
Async XLA Ops:
  0.6 26.6 %copy-start.1 = (bf16[3,256,512]{2,1,0:T(8,128)(2,1)S(1)}, bf16[3,256,512]{2,1,0:T(8,128)(2,1)}, u32[]{:S(2)}) copy-start(bf16[3,256,512]{2,1,0:T(8,128)(2,1)} %param.8) | copy-start | bytes 2359300
  24.3 12.8 %copy-start.5 = (s32[69]{0:T(128)S(1)}, s32[69]{0:T(128)}, u32[]{:S(2)}) copy-start(s32[69]{0:T(128)} %param.9) | copy-start | bytes 832
  24.3 12.9 %collective-permute-start = (bf16[69,2,128]{0,2,1:T(8,128)(2,1)S(1)}, bf16[69,2,128]{0,2,1:T(8,128)(2,1)S(1)}, u32[]{:S(2)}, u32[]{:S(2)}) collective-permute-start(bf16[69,2,128]{0,2,1:T(8,128)(2,1)S(1)} %get-tuple-element.16), channel_id=1, source_target_pairs={{0,4},{4,8},{8,12},{12,16},{16,20},{20,24},{24,28},{1,5},{5,9},{9,... | collective-permute-start | bytes 105992 | tf_op jit(solution)/shard_map/ppermute | solution.py:19
  26.0 11.2 %collective-permute-start.1 = (bf16[69,2,128]{0,2,1:T(8,128)(2,1)S(1)}, bf16[69,2,128]{0,2,1:T(8,128)(2,1)S(1)}, u32[]{:S(2)}, u32[]{:S(2)}) collective-permute-start(bf16[69,2,128]{0,2,1:T(8,128)(2,1)S(1)} %get-tuple-element.17), channel_id=1, source_target_pairs={{4,0},{8,4},{12,8},{16,12},{20,16},{24,20},{28,24},{5,1},{9,5},{13... | collective-permute-start | bytes 105992 | tf_op jit(solution)/shard_map/ppermute | solution.py:22
  28.6 29.2 %copy-start.2 = (bf16[9,256,69]{1,2,0:T(8,128)(2,1)S(1)}, bf16[9,256,69]{1,2,0:T(8,128)(2,1)}, u32[]{:S(2)}) copy-start(bf16[9,256,69]{1,2,0:T(8,128)(2,1)} %param.10) | copy-start | bytes 953860
  28.6 96.8 %all-to-all-start = ((bf16[32,3,32,128]{3,2,1,0:T(8,128)(2,1)}), bf16[32,3,32,128]{3,2,1,0:T(8,128)(2,1)}, u32[]{:S(2)}, u32[]{:S(2)}) async-start(bf16[32,3,32,128]{3,2,1,0:T(8,128)(2,1)} %bitcast.39), calls=%async_computation | async-start | bytes 1572864 | tf_op jit(solution)/shard_map/all_to_all | solution.py:47
  37.3 20.0 %collective-permute-start.3 = (bf16[69,36,2]{0,2,1:T(2,128)(2,1)S(1)}, bf16[69,36,2]{0,2,1:T(2,128)(2,1)S(1)}, u32[]{:S(2)}, u32[]{:S(2)}) collective-permute-start(bf16[69,36,2]{0,2,1:T(2,128)(2,1)S(1)} %get-tuple-element.15), channel_id=1, source_target_pairs={{1,0},{2,1},{3,2},{0,3},{5,4},{6,5},{7,6},{4,7},{9,8},{10,9},{11,1... | collective-permute-start | bytes 29816 | tf_op jit(solution)/shard_map/ppermute | solution.py:22
  37.6 19.6 %collective-permute-start.2 = (bf16[69,36,2]{0,2,1:T(2,128)(2,1)S(1)}, bf16[69,36,2]{0,2,1:T(2,128)(2,1)S(1)}, u32[]{:S(2)}, u32[]{:S(2)}) collective-permute-start(bf16[69,36,2]{0,2,1:T(2,128)(2,1)S(1)} %get-tuple-element.14), channel_id=1, source_target_pairs={{0,1},{1,2},{2,3},{3,0},{4,5},{5,6},{6,7},{7,4},{8,9},{9,10},{10,1... | collective-permute-start | bytes 29816 | tf_op jit(solution)/shard_map/ppermute | solution.py:19
  76.2 2.9 %copy-start.3 = (f32[256]{0:T(256)S(1)}, f32[256]{0:T(256)}, u32[]{:S(2)}) copy-start(f32[256]{0:T(256)} %param.11) | copy-start | bytes 3076
  79.1 12.7 %copy-start = (bf16[9,256,256]{2,1,0:T(8,128)(2,1)S(1)}, bf16[9,256,256]{2,1,0:T(8,128)(2,1)}, u32[]{:S(2)}) copy-start(bf16[9,256,256]{2,1,0:T(8,128)(2,1)} %param.12) | copy-start | bytes 3538948
  108.8 2.7 %copy-start.4 = (f32[256]{0:T(256)S(1)}, f32[256]{0:T(256)}, u32[]{:S(2)}) copy-start(f32[256]{0:T(256)} %param.13) | copy-start | bytes 3076
